TPU v7x, 32 devices: a whole 2x2x4 slice. The times are simulated.
32 devices in a mesh: blk: 8 (over z, y), tp: 4 (over x, core).
Axes of the slice: x: 2, y: 2, z: 4, core: 2. Of those that a mesh axis runs over, the one named last changes fastest.
Arguments:
- tokens: bfloat16 [2048, 2048], P('blk'), may hold values from -27 to 27
- order: int32 [16], replicated, may hold values from 0 to 15, each once
- gain_attn: float32 [2048], replicated, may hold values from 0.1 to 1.9
- gain_ffn: float32 [2048], replicated, may hold values from 0.1 to 1.9
- w_query: bfloat16 [2048, 2048], P(None, 'tp'), may hold values from -3.7565048 to 3.7565048
- w_key: bfloat16 [2048, 512], P(None, 'tp'), may hold values from -0.13258252 to 0.13258252
- w_value: bfloat16 [2048, 512], P(None, 'tp'), may hold values from -0.125 to 0.125
- w_out: bfloat16 [2048, 2048], P('tp'), may hold values from -0.125 to 0.125
- w_gate: bfloat16 [2048, 8192], P(None, 'tp'), may hold values from -0.125 to 0.125
- w_up: bfloat16 [2048, 8192], P(None, 'tp'), may hold values from -0.125 to 0.125
- w_down: bfloat16 [8192, 2048], P('tp'), may hold values from -0.0625 to 0.0625
Outputs:
- layer_out: bfloat16 [2048, 2048], P('blk', 'tp')
Inputs may be any that keep to these rules, and one draw needn't show every extreme that they name: `order`: every number 0 to 15 appears once; device b of blk holds stored blocks 2b and 2b + 1.
All inputs are finite; a program needn't handle non-finite values.
Results may differ from a plain program's by a relative error of at most 0.0095.
Values may be sent and summed in bfloat16 or wider, within the bound.
A program may use at most 128 MiB of HBM per device.

v0:
```python
import jax
import jax.numpy as jnp
from jax import lax
from jax.sharding import PartitionSpec as P

HD = 64


EPS = 1e-05
ROPE_BASE = 500000.0
MASKED = -1e30


def rotate(values, positions):
    half_dim = values.shape[-1] // 2
    freq = ROPE_BASE ** (-(jnp.arange(half_dim, dtype=jnp.float32) * 2.0 / values.shape[-1]))
    angle = positions.astype(jnp.float32)[:, None] * freq[None, :]
    cosine = jnp.cos(angle)[:, None, :]
    sine = jnp.sin(angle)[:, None, :]
    first = values[..., :half_dim]
    second = values[..., half_dim:]
    return jnp.concatenate(
        [first * cosine - second * sine, second * cosine + first * sine], axis=-1
    )


def stored_positions(order, start, count, half_rows):
    stored = start + jnp.arange(count, dtype=jnp.int32)
    which = stored // half_rows
    match = which[:, None] == jnp.arange(order.shape[0], dtype=jnp.int32)[None, :]
    first = jnp.sum(jnp.where(match, order[None, :], 0), axis=1)
    return first * half_rows + stored % half_rows


def local(tokens, order, gain_attn, gain_ffn, w_query, w_key, w_value, w_out, w_gate, w_up, w_down):
    tok_rows, model_width = tokens.shape
    half_rows = tok_rows // 2
    kv_local = w_key.shape[1] // HD
    query_local = w_query.shape[1] // HD
    group = query_local // kv_local
    score_scale = HD ** (-0.5)
    query_pos = stored_positions(order, lax.axis_index("blk") * tok_rows, tok_rows, half_rows)
    tokens_wide = tokens.astype(jnp.float32)
    normed = (
        tokens_wide
        * lax.rsqrt(jnp.mean(tokens_wide * tokens_wide, axis=-1, keepdims=True) + EPS)
        * gain_attn
    ).astype(jnp.bfloat16)
    queries = jnp.dot(normed, w_query, preferred_element_type=jnp.float32).reshape(
        tok_rows, query_local, HD
    )
    queries = rotate(queries, query_pos).astype(jnp.bfloat16).reshape(tok_rows, kv_local, group, HD)
    keys = jnp.dot(normed, w_key, preferred_element_type=jnp.float32).reshape(
        tok_rows, kv_local, HD
    )
    keys = rotate(keys, query_pos).astype(jnp.bfloat16)
    values = jnp.dot(normed, w_value, preferred_element_type=jnp.float32).astype(jnp.bfloat16)
    packed = jnp.concatenate([keys.reshape(tok_rows, kv_local * HD), values], axis=1)

    def attend(carry, block, key_pos):
        running, denominator, accum = carry
        key_block = block[:, : kv_local * HD].reshape(-1, kv_local, HD)
        value_block = block[:, kv_local * HD :].reshape(-1, kv_local, HD)
        scores = (
            jnp.einsum("qkgd,skd->kgqs", queries, key_block, preferred_element_type=jnp.float32)
            * score_scale
        )
        allowed = key_pos[None, :] <= query_pos[:, None]
        scores = jnp.where(allowed, scores, MASKED)
        newest = jnp.maximum(running, jnp.max(scores, axis=-1))
        weights = jnp.where(allowed, jnp.exp(scores - newest[..., None]), 0.0)
        factor = jnp.exp(running - newest)
        denominator = denominator * factor + jnp.sum(weights, axis=-1)
        accum = accum * factor[..., None] + jnp.einsum(
            "kgqs,skd->kgqd",
            weights.astype(jnp.bfloat16),
            value_block,
            preferred_element_type=jnp.float32,
        )
        return (newest, denominator, accum)

    def consider(carry, block, key_pos):
        return attend(carry, block, key_pos)

    start_carry = (
        jnp.full((kv_local, group, tok_rows), MASKED, jnp.float32),
        jnp.zeros((kv_local, group, tok_rows), jnp.float32),
        jnp.zeros((kv_local, group, tok_rows, HD), jnp.float32),
    )
    piece = lax.all_gather(packed, "blk", axis=0, tiled=True)
    count = piece.shape[0]
    key_pos = stored_positions(order, jnp.int32(0), count, half_rows)
    turns = min(16, count // 512)
    size = count // turns

    def one_turn(turn, inner):
        offset = turn * size
        return consider(
            inner,
            lax.dynamic_slice_in_dim(piece, offset, size, 0),
            lax.dynamic_slice_in_dim(key_pos, offset, size, 0),
        )

    running, denominator, accum = lax.fori_loop(0, turns, one_turn, start_carry)
    heads = (accum / denominator[..., None]).astype(jnp.bfloat16)
    heads = jnp.transpose(heads, (2, 0, 1, 3)).reshape(tok_rows, query_local * HD)
    partial_value = jnp.dot(heads, w_out, preferred_element_type=jnp.float32)
    share = model_width // lax.axis_size("tp")
    col_start = lax.axis_index("tp") * share
    attention = lax.psum(partial_value.astype(jnp.bfloat16), "tp").astype(jnp.float32)
    resid_full = tokens_wide + attention
    normed_ffn = (
        resid_full
        * lax.rsqrt(jnp.mean(resid_full * resid_full, axis=-1, keepdims=True) + EPS)
        * gain_ffn
    ).astype(jnp.bfloat16)
    gate = jnp.dot(normed_ffn, w_gate, preferred_element_type=jnp.float32)
    up_proj = jnp.dot(normed_ffn, w_up, preferred_element_type=jnp.float32)
    residual = lax.dynamic_slice_in_dim(resid_full, col_start, share, 1)
    hidden = (jax.nn.silu(gate) * up_proj).astype(jnp.bfloat16)
    down = jnp.dot(hidden, w_down, preferred_element_type=jnp.float32)
    feed = lax.psum_scatter(
        down.astype(jnp.bfloat16), "tp", scatter_dimension=1, tiled=True
    ).astype(jnp.float32)
    return (residual + feed).astype(jnp.bfloat16)


def solution(mesh):
    placed = (
        P("blk", None),
        P(),
        P(),
        P(),
        P(None, "tp"),
        P(None, "tp"),
        P(None, "tp"),
        P("tp", None),
        P(None, "tp"),
        P(None, "tp"),
        P("tp", None),
    )
    return jax.shard_map(
        local, mesh=mesh, in_specs=placed, out_specs=P("blk", "tp"), check_vma=False
    )
```

profile of v0, /device:TPU:0, one launch (start us, length us, event | category | flops | bytes accessed | tf_op | source)
XLA Modules:
  0.0 170.3 jit_solution(14542526283419037584)
XLA Ops:
  6.6 1.7 fusion.14
  8.3 0.8 select_reduce_fusion.1
  9.1 1.9 %convolution_convert_fusion.2 = bf16[256,128]{0,1:T(8,128)(2,1)S(1)} fusion(bf16[2048,128]{1,0:T(8,128)(2,1)} %param.19, bf16[256,2048]{1,0:T(8,128)(2,1)} %param.13, f32[2048]{0:T(1024)} %param.15, f32[256]{0:T(256)S(1)} %add_rsqrt_fusion.1), kind=kOutput, calls=%fused_computation.30 | convolution fusion | flops 136347648 | bytes 1647616 | tf_op jit(solution)/shard_map/dot_general | solution.py:57
  11.1 0.6 fusion.32
  11.7 0.2 multiply_cosine_fusion
  11.9 0.7 pad_maximum_fusion.1
  12.7 0.1 select_reduce_fusion
  12.8 2.6 %fusion.29 = f32[256,512]{0,1:T(8,128)S(1)} fusion(bf16[2048,512]{1,0:T(8,128)(2,1)} %param.17, bf16[256,2048]{1,0:T(8,128)(2,1)S(1)} %copy-done.1, f32[2048]{0:T(1024)S(1)} %copy-done.7, f32[256]{0:T(256)S(1)} %add_rsqrt_fusion.1), kind=kOutput, calls=%fused_computation.72 | convolution fusion | flops 538968064 | bytes 3679232 | tf_op jit(solution)/shard_map/dot_general | solution.py:49
  15.4 0.1 subtract_convert_fusion
  15.5 39.3 %all-gather.2.cloned.1.call-done = bf16[2048,256]{0,1:T(8,128)(2,1)} async-done(((bf16[256,256]{0,1:T(8,128)(2,1)}), bf16[2048,256]{0,1:T(8,128)(2,1)}) %all-gather.2.cloned.1.call-update) | async-done | bytes 1048592 | tf_op jit(solution)/shard_map/all_gather | solution.py:90
  54.9 20.8 %while.18 = (s32[]{:T(128)}, f32[2,4,256]{2,1,0:T(4,128)S(1)}, f32[2,4,256]{2,1,0:T(4,128)S(1)}, f32[2,4,256,64]{2,3,1,0:T(8,128)}, s32[2048]{0:T(1024)S(1)}, /*...) while((s32[]{:T(128)}, f32[2,4,256]{2,1,0:T(4,128)S(1)}, ...), condition=%wide.region_6.7_spmd.clone, body=%wide.region_3.6_spmd.clone.sunk | while | flops 282601472 | bytes 19537168 | solution.py:104
  54.9 0.1 dynamic_slice.22
  55.0 0.1 broadcast_compare_fusion.3
  55.1 1.0 fusion.61
  56.1 0.8 fusion.62
  56.9 1.0 fusion.63
  58.0 1.3 fusion.65
  59.3 0.8 copy-done.4
  60.1 0.1 dynamic_slice.22
  60.2 0.1 broadcast_compare_fusion.3
  60.3 1.0 fusion.61
  61.3 0.8 fusion.62
  62.1 1.0 fusion.63
  63.2 1.3 fusion.65
  64.5 0.8 copy-done.4
  65.3 0.1 dynamic_slice.22
  65.3 0.1 broadcast_compare_fusion.3
  65.5 1.0 fusion.61
  66.5 0.8 fusion.62
  67.3 1.0 fusion.63
  68.4 1.3 fusion.65
  69.7 0.8 copy-done.4
  70.5 0.1 dynamic_slice.22
  70.5 0.1 broadcast_compare_fusion.3
  70.7 1.0 fusion.61
  71.7 0.8 fusion.62
  72.5 1.0 fusion.63
  73.6 1.3 fusion.65
  74.9 0.8 copy-done.4
  75.7 1.1 divide_convert_fusion
  76.8 1.7 convolution_convert_fusion
  78.5 0.2 reduce-scatter.2.cloned.1.call-start
  78.7 35.2 %all-reduce.2.cloned.1.call-done = bf16[256,2048]{1,0:T(8,128)(2,1)} async-done(((bf16[256,2048]{1,0:T(8,128)(2,1)}), bf16[256,2048]{1,0:T(8,128)(2,1)}) %all-reduce.2.cloned.1.call-update) | async-done | bytes 1048592 | tf_op jit(solution)/shard_map/psum | solution.py:110
  113.9 3.0 %convert_add_fusion = (f32[256,2048]{1,0:T(8,128)}, f32[256]{0:T(256)S(1)}) fusion(bf16[256,2048]{1,0:T(8,128)(2,1)S(1)} %copy-done.1, bf16[256,2048]{1,0:T(8,128)(2,1)} %all-reduce.2.cloned.1.call-done), kind=kLoop, calls=%fused_computation.18 | loop fusion | flops 2621184 | bytes 4195328 | tf_op jit(solution)/shard_map/add | solution.py:111
  116.9 7.1 %fusion.28 = f32[256,2048]{1,0:T(8,128)} fusion(bf16[2048,2048]{1,0:T(8,128)(2,1)} %param.21, f32[2048]{0:T(1024)S(1)} %copy-done.8, f32[256]{0:T(256)S(1)} %add_rsqrt_fusion, bf16[256,2048]{1,0:T(8,128)(2,1)S(1)} %copy-done.1, bf16[256,2048]{1,0:T(8,128)(2,1)S(1)} %copy-done.2), kind=kOutput, calls=%fused_computation.71 | convolution fusion | flops 2150629376 | bytes 12592128 | tf_op jit(solution)/shard_map/dot_general | solution.py:117
  124.1 12.4 %convolution_convert_fusion.1 = bf16[256,2048]{1,0:T(8,128)(2,1)} fusion(bf16[2048,2048]{1,0:T(8,128)(2,1)} %param.23, bf16[2048,2048]{1,0:T(8,128)(2,1)} %param.22, f32[256,2048]{1,0:T(8,128)} %fusion.28, f32[2048]{0:T(1024)S(1)} %copy-done.8, f32[256]{0:T(256)S(1)} %add_rsqrt_fusion, bf16[256,2048]{1,0:T(8,128)(2,1)S(1)} %copy-done.1, ...), kind=kOutput, calls=%fused_computation.24 | convolution fusion | flops 4301783040 | bytes 22029312 | tf_op jit(solution)/shard_map/dot_general | solution.py:121
  136.5 25.4 %reduce-scatter.2.cloned.1.call-done = bf16[256,512]{1,0:T(8,128)(2,1)} async-done(((bf16[256,2048]{1,0:T(8,128)(2,1)}), bf16[256,512]{1,0:T(8,128)(2,1)}) %reduce-scatter.2.cloned.1.call-update) | async-done | bytes 262160 | tf_op jit(solution)/shard_map/reduce_scatter | solution.py:122
  161.9 1.9 %add_convert_fusion = bf16[256,512]{1,0:T(8,128)(2,1)} fusion(bf16[256,512]{1,0:T(8,128)(2,1)} %reduce-scatter.2.cloned.1.call-done, f32[256,2048]{1,0:T(8,128)} %get-tuple-element.198, s32[]{:T(128)S(6)} %select_n.75), kind=kLoop, calls=%fused_computation.31 | loop fusion | flops 393216 | bytes 1048580 | tf_op jit(solution)/shard_map/convert_element_type | solution.py:125
  (56 shorter events, 0.4 us)
Async XLA Ops:
  6.5 70.2 %copy-start = (bf16[512,2048]{1,0:T(8,128)(2,1)S(1)}, bf16[512,2048]{1,0:T(8,128)(2,1)}, u32[]{:S(2)}) copy-start(bf16[512,2048]{1,0:T(8,128)(2,1)} %param.20) | copy-start | bytes 6291460
  6.5 4.5 %copy-start.1 = (bf16[256,2048]{1,0:T(8,128)(2,1)S(1)}, bf16[256,2048]{1,0:T(8,128)(2,1)}, u32[]{:S(2)}) copy-start(bf16[256,2048]{1,0:T(8,128)(2,1)} %param.13) | copy-start | bytes 3145732
  6.5 4.5 %copy-start.7 = (f32[2048]{0:T(1024)S(1)}, f32[2048]{0:T(1024)}, u32[]{:S(2)}) copy-start(f32[2048]{0:T(1024)} %param.15) | copy-start | bytes 24580
  6.5 48.3 %all-gather.2.cloned.1.call-start = ((), (), s32[]{:S(2)}) async-start(), calls=%async_computation.1 | async-start | bytes 1179648 | tf_op jit(solution)/shard_map/all_gather | solution.py:90
  8.2 2.8 %copy-start.6 = (bf16[2048,128]{1,0:T(8,128)(2,1)S(1)}, bf16[2048,128]{1,0:T(8,128)(2,1)}, u32[]{:S(2)}) copy-start(bf16[2048,128]{1,0:T(8,128)(2,1)} %param.18) | copy-start | bytes 1572868
  11.1 1.6 copy-start.5
  12.6 101.3 %all-reduce.2.cloned.1.call-start = ((), (), s32[]{:S(2)}) async-start(), calls=%async_computation.2 | async-start | bytes 2097152 | tf_op jit(solution)/shard_map/psum | solution.py:110
  56.9 1.0 copy-start.3
  59.3 0.8 copy-start.4
  62.1 1.0 copy-start.3
  64.5 0.8 copy-start.4
  67.3 1.0 copy-start.3
  69.7 0.8 copy-start.4
  72.5 1.0 copy-start.3
  74.9 0.8 copy-start.4
  78.5 38.4 %copy-start.8 = (f32[2048]{0:T(1024)S(1)}, f32[2048]{0:T(1024)}, u32[]{:S(2)}) copy-start(f32[2048]{0:T(1024)} %param.16) | copy-start | bytes 24580
  78.5 83.4 %reduce-scatter.2.cloned.1.call-start = ((), (), s32[]{:S(2)}) async-start(), calls=%async_computation.3 | async-start | bytes 1310720 | tf_op jit(solution)/shard_map/reduce_scatter | solution.py:122
  113.9 3.0 %copy-start.2 = (bf16[256,2048]{1,0:T(8,128)(2,1)S(1)}, bf16[256,2048]{1,0:T(8,128)(2,1)}, u32[]{:S(2)}) copy-start(bf16[256,2048]{1,0:T(8,128)(2,1)} %all-reduce.2.cloned.1.call-done) | copy-start | bytes 3145732
Sparse Core Ops, SparseCore 0:
  12.7 42.1 all-gather.1
  78.6 35.2 all-reduce.1
  136.6 25.2 reduce-scatter.1
where the time goes:
time: 171 us; the launch traced here: 170 us
  waiting for transfers between devices  100 us (58%)
  matrix products  34.7 us (20%)
  other arithmetic  14.3 us (8%)
  between operations  13.3 us (8%)
  local copies, waits for them, and re-layouts  7.5 us (4%)
    all_gather x1, waiting for transfers between devices, local(): piece = lax.all_gather(packed, 'blk', axis=0, tiled=True)  39.3 us
    psum x1, waiting for transfers between devices, local(): lax.psum(partial_value.astype(jnp.bfloat16), 'tp').astype(jnp.float32)  35.2 us
    reduce_scatter x1, waiting for transfers between devices, local(): lax.psum_scatter(down.astype(jnp.bfloat16), 'tp', scatter_dimension=1, ti...  25.4 us
    dot_general x1, matrix products, local(): down = jnp.dot(hidden, w_down, preferred_element_type=jnp.float32)  12.4 us
    dot_general x1, matrix products, local(): gate = jnp.dot(normed_ffn, w_gate, preferred_element_type=jnp.float32)  7.14 us
    dot_general x4, matrix products, attend(): jnp.einsum('kgqs,skd->kgqd', weights.astype(jnp.bfloat16), value_block, p...  5.08 us
    reduce_sum x4, other arithmetic, attend(): denominator = denominator * factor + jnp.sum(weights, axis=-1)  4.03 us
    slice x4, local copies, waits for them, and re-layouts, attend(): value_block = block[:, kv_local * HD:].reshape(-1, kv_local, HD)  3.98 us
  transfers between devices with their start and end apart: 3, of which 3 were waited for; matrix products, arithmetic and copies ran while one was open for 2% of the time, Pallas kernels for 0%

commit v1 on v0

v1 whole, which is shorter than its diff:
```python
import functools

import jax
import jax.numpy as jnp
from jax import lax
from jax.experimental import pallas as pl
from jax.experimental.pallas import tpu as pltpu
from jax.sharding import PartitionSpec as P

HD = 64
EPS = 1e-05
ROPE_BASE = 500000.0
MASKED = -1e30
MESH = pl.DeviceIdType.MESH
CHUNKS = 2
BF = jnp.bfloat16
F32 = jnp.float32


def dot(a, b):
    return jnp.dot(a, b, preferred_element_type=F32)


def ring_place(index, n):
    z, y = index // 2, index % 2
    return y * (n - 1 - z) + (1 - y) * z


def ring_index(place, n):
    place = lax.rem(place + 2 * n, n)
    far = place // (n // 2)
    return far * (2 * (n - 1 - place) + 1) + (1 - far) * (2 * place)


def kernel(
    n,
    tokens, gain_attn, gain_ffn, cosine, sine, qpos, kpos,
    w_query, w_key, w_value, w_out, w_gate, w_up, w_down,
    out,
    wq, wkv, wo, wg, wu, wd,
    normed, q_v, kv, m_v, acc, heads, resid, hidden, fin,
    p_send, p_recv, cs_mine, cs_peer, xr_mine, xr_peer,
    rs_send, rs_recv, xs_send, xs_recv,
    wsem, ksend, krecv, asend, arecv,
):
    rows, width = tokens.shape
    n_heads = q_v.shape[0]
    group = n_heads // 2
    half = width // 2
    share = width // 4
    blk = lax.axis_index("blk")
    tp = lax.axis_index("tp")
    core = lax.rem(tp, 2)
    xx = tp // 2
    peer = xx * 2 + (1 - core)
    across = (1 - xx) * 2 + core
    place = ring_place(blk, n)
    right = ring_index(place + 1, n)
    left = ring_index(place - 1, n)

    def load(src, dst, k):
        return pltpu.make_async_copy(src, dst, wsem.at[k])

    first = [
        load(w_key, wkv.at[:, 0:128], 0),
        load(w_value, wkv.at[:, 128:256], 1),
        load(w_query, wq, 2),
    ]
    for c in first:
        c.start()
    barrier = pltpu.get_barrier_semaphore()
    for target in ({"blk": right}, {"blk": left}, {"tp": peer}, {"tp": across}):
        pl.semaphore_signal(barrier, inc=1, device_id=target, device_id_type=MESH)

    wide = tokens[...].astype(F32)
    scale = lax.rsqrt(jnp.mean(wide * wide, axis=-1, keepdims=True) + EPS)
    normed[...] = (wide * scale * gain_attn[...]).astype(BF)

    lane = lax.broadcasted_iota(jnp.int32, (rows, 128), 1)
    low = lane < 64
    rope_first = (lane % 64) < 32

    def rope(u):
        turned = jnp.where(rope_first, pltpu.roll(u, 96, 1), pltpu.roll(u, 32, 1))
        return u * cosine[...] + turned * sine[...]

    first[0].wait()
    first[1].wait()
    rest = []
    for g in range(group):
        for b in range(2):
            rest.append(
                load(
                    w_out.at[pl.ds((b * group + g) * HD, HD)],
                    wo.at[pl.ds((2 * g + b) * HD, HD)],
                    6 + 2 * g + b,
                )
            )
    rest_ffn = [load(w_gate, wg, 3), load(w_up, wu, 4), load(w_down, wd, 5)]
    for c in rest:
        c.start()
    for c in rest_ffn:
        c.start()
    kv_new = dot(normed[...], wkv[...])
    kv[blk, :, 0:128] = rope(kv_new[:, 0:128]).astype(BF)
    kv[blk, :, 128:256] = kv_new[:, 128:256].astype(BF)
    pl.semaphore_wait(barrier, 4)

    hop = n // 2
    hrow = rows // 2

    def ring_copy(direction, step, part):
        toward = right if direction == 0 else left
        owner = ring_index(place - (step - 1) if direction == 0 else place + (step - 1), n)
        ref = kv.at[owner, pl.ds(part * hrow, hrow)]
        k = (direction * hop + step - 1) * 2 + part
        return pltpu.make_async_remote_copy(
            src_ref=ref, dst_ref=ref,
            send_sem=ksend.at[k], recv_sem=krecv.at[k],
            device_id={"blk": toward}, device_id_type=MESH,
        )

    def arrival(direction, step, part):
        owner = ring_index(place - step if direction == 0 else place + step, n)
        ref = kv.at[owner, pl.ds(part * hrow, hrow)]
        k = (direction * hop + step - 1) * 2 + part
        return pltpu.make_async_remote_copy(
            src_ref=ref, dst_ref=ref,
            send_sem=ksend.at[k], recv_sem=krecv.at[k],
            device_id={"blk": right if direction == 0 else left}, device_id_type=MESH,
        )

    def used(direction, step, part):
        return step < hop or part == direction

    sent = []

    def send(direction, step, part):
        if step <= hop and used(direction, step, part):
            c = ring_copy(direction, step, part)
            c.start()
            sent.append(c)

    for part in range(2):
        for direction in range(2):
            send(direction, 1, part)

    first[2].wait()
    for i in range(n_heads // 2):
        u = rope(dot(normed[...], wq[:, i * 128:(i + 1) * 128])) * (HD ** -0.5)
        turned = pltpu.roll(u, 64, 1)
        for b in range(2):
            j = 2 * i + b
            upper = j // group
            picked = u if upper == b else turned
            keep = low if upper == 0 else jnp.logical_not(low)
            q_v[j] = jnp.where(keep, picked, 0.0).astype(BF)

    def attend(blocks, fresh):
        biases = [
            jnp.where(kpos[b] <= qpos[...], 0.0, MASKED).astype(F32) for b in blocks
        ]
        ones = jnp.ones((rows, 128), BF)

        for j in range(n_heads):
            upper = j // group
            parts = [
                lax.dot_general(
                    q_v[j], kv[b, :, 0:128], (((1,), (1,)), ((), ())),
                    preferred_element_type=F32,
                ) + bias
                for b, bias in zip(blocks, biases)
            ]
            top = functools.reduce(
                jnp.maximum, [jnp.max(s, axis=1, keepdims=True) for s in parts]
            )
            if fresh:
                newest = jnp.broadcast_to(top, (rows, 128))
            else:
                old = m_v[j]
                newest = jnp.maximum(old, top)
            both = jnp.concatenate([newest] * (rows // 128), axis=1)
            total = None
            for b, s in zip(blocks, parts):
                vals = kv[b, :, 128:256]
                aug = jnp.where(low, vals, ones) if upper == 0 else jnp.where(low, ones, vals)
                d = dot(jnp.exp(s - both).astype(BF), aug)
                total = d if total is None else total + d
            if fresh:
                acc[j] = total
            else:
                acc[j] = acc[j] * jnp.exp(old - newest) + total
            m_v[j] = newest

    attend([blk], True)
    for step in range(1, hop + 1):
        for part in range(2):
            for direction in range(2):
                if used(direction, step, part):
                    arrival(direction, step, part).wait_recv()
                    send(direction, step + 1, part)
        if step < hop:
            attend([ring_index(place - step, n), ring_index(place + step, n)], False)
        else:
            attend([ring_index(place + step, n)], False)

    for g in range(group):
        a, b = acc[g], acc[group + g]
        a = a / pltpu.roll(a, 64, 1)
        b = b / pltpu.roll(b, 64, 1)
        heads[:, g * 128:(g + 1) * 128] = jnp.where(low, a, b).astype(BF)
    for c in rest:
        c.wait()

    count = rows // CHUNKS
    mine = pl.multiple_of(core * half, half)
    theirs = pl.multiple_of((1 - core) * half, half)
    span = [pl.ds(c * count, count) for c in range(CHUNKS)]

    def move(src, dst, k, c, target):
        return pltpu.make_async_remote_copy(
            src_ref=src, dst_ref=dst,
            send_sem=asend.at[k * CHUNKS + c], recv_sem=arecv.at[k * CHUNKS + c],
            device_id={"tp": target}, device_id_type=MESH,
        )

    give = [move(p_send.at[s], p_recv.at[s], 0, c, peer) for c, s in enumerate(span)]
    cross = [move(cs_mine.at[s], xr_mine.at[s], 1, c, across) for c, s in enumerate(span)]
    share_cs = [move(cs_mine.at[s], cs_peer.at[s], 2, c, peer) for c, s in enumerate(span)]
    forward = [move(xr_mine.at[s], xr_peer.at[s], 3, c, peer) for c, s in enumerate(span)]
    down_far = [
        move(rs_send.at[0, s], rs_recv.at[0, s], 4, c, peer) for c, s in enumerate(span)
    ]
    down_near = [
        move(rs_send.at[1, s], rs_recv.at[1, s], 5, c, peer) for c, s in enumerate(span)
    ]
    down_cross = [move(xs_send.at[s], xs_recv.at[s], 6, c, across) for c, s in enumerate(span)]

    for c, s in enumerate(span):
        p_send[s] = dot(heads[s], wo[:, pl.ds(theirs, half)]).astype(BF)
        give[c].start()
    for c, s in enumerate(span):
        own = dot(heads[s], wo[:, pl.ds(mine, half)]).astype(BF).astype(F32)
        give[c].wait_recv()
        cs_mine[s] = (own + p_recv[s].astype(F32)).astype(BF)
        cross[c].start()
        share_cs[c].start()

    def quarter(x_of, core_of):
        return pl.ds(pl.multiple_of((x_of * 2 + core_of) * share, share), share)

    for c, s in enumerate(span):
        cross[c].wait_recv()
        forward[c].start()
        a = tokens[s, pl.ds(mine, half)].astype(F32) + (
            cs_mine[s].astype(F32) + xr_mine[s].astype(F32)
        )
        resid[s, pl.ds(mine, half)] = a
        share_cs[c].wait_recv()
        forward[c].wait_recv()
        b = tokens[s, pl.ds(theirs, half)].astype(F32) + (
            cs_peer[s].astype(F32) + xr_peer[s].astype(F32)
        )
        resid[s, pl.ds(theirs, half)] = b
        square = jnp.sum(a * a, axis=-1, keepdims=True) + jnp.sum(b * b, axis=-1, keepdims=True)
        factor = lax.rsqrt(square / width + EPS)
        normed[s] = (resid[s] * factor * gain_ffn[...]).astype(BF)
        if c == 0:
            rest_ffn[0].wait()
            rest_ffn[1].wait()

        tile = 512

        @pl.loop(0, hidden.shape[1] // tile)
        def _(t):
            cols = pl.ds(pl.multiple_of(t * tile, tile), tile)
            gate = dot(normed[s], wg[:, cols])
            up = dot(normed[s], wu[:, cols])
            hidden[s, cols] = (gate / (1.0 + jnp.exp(-gate)) * up).astype(BF)

        if c == 0:
            rest_ffn[2].wait()
        rs_send[0, s] = dot(hidden[s], wd[:, quarter(1 - xx, 1 - core)]).astype(BF)
        down_far[c].start()
        own = dot(hidden[s], wd[:, quarter(1 - xx, core)]).astype(BF).astype(F32)
        down_far[c].wait_recv()
        xs_send[s] = (own + rs_recv[0, s].astype(F32)).astype(BF)
        down_cross[c].start()
        rs_send[1, s] = dot(hidden[s], wd[:, quarter(xx, 1 - core)]).astype(BF)
        down_near[c].start()
        own = dot(hidden[s], wd[:, quarter(xx, core)]).astype(BF).astype(F32)
        down_near[c].wait_recv()
        fin[s] = resid[s, quarter(xx, core)] + (own + rs_recv[1, s].astype(F32))
    for c, s in enumerate(span):
        down_cross[c].wait_recv()
        out[s] = (fin[s] + xs_recv[s].astype(F32)).astype(BF)
    for c in sent:
        c.wait_send()
    for c in range(CHUNKS):
        for group_of in (give, cross, share_cs, forward, down_far, down_near, down_cross):
            group_of[c].wait_send()


def local(n, tokens, order, gain_attn, gain_ffn, w_query, w_key, w_value, w_out, w_gate, w_up, w_down):
    rows, width = tokens.shape
    half_rows = rows // 2
    inner = w_query.shape[1]
    n_heads = inner // HD
    ffn = w_gate.shape[1]
    count = n * rows
    positions = (order[:, None] * half_rows + jnp.arange(half_rows, dtype=jnp.int32)[None, :]).reshape(
        n, 1, rows
    )
    blk = lax.axis_index("blk")
    query_pos = lax.dynamic_slice_in_dim(positions, blk, 1, 0).reshape(rows, 1)
    lanes = jnp.arange(128, dtype=jnp.int32)
    freq = ROPE_BASE ** (-((lanes % 32).astype(F32) * 2.0 / HD))
    angle = query_pos.astype(F32) * freq[None, :]
    cosine = jnp.cos(angle)
    sine = jnp.sin(angle) * jnp.where((lanes % HD) < HD // 2, -1.0, 1.0)[None, :]
    vmem = pl.BlockSpec(memory_space=pltpu.VMEM)
    hbm = pl.BlockSpec(memory_space=pl.ANY)
    V = pltpu.VMEM
    hop = n // 2
    return pl.pallas_call(
        functools.partial(kernel, n),
        out_shape=jax.ShapeDtypeStruct((rows, width // 4), BF),
        in_specs=[vmem] * 7 + [hbm] * 7,
        out_specs=vmem,
        scratch_shapes=[
            V((width, inner), BF), V((width, 256), BF), V((inner, width), BF),
            V((width, ffn), BF), V((width, ffn), BF), V((ffn, width), BF),
            V((rows, width), BF), V((n_heads, rows, 128), BF), V((n, rows, 256), BF),
            V((n_heads, rows, 128), F32), V((n_heads, rows, 128), F32),
            V((rows, inner), BF), V((rows, width), F32), V((rows, ffn), BF),
            V((rows, width // 4), F32),
        ]
        + [V((rows, width // 2), BF)] * 6
        + [
            V((2, rows, width // 4), BF), V((2, rows, width // 4), BF),
            V((rows, width // 4), BF), V((rows, width // 4), BF),
            pltpu.SemaphoreType.DMA((6 + n_heads,)),
            pltpu.SemaphoreType.DMA((4 * hop,)), pltpu.SemaphoreType.DMA((4 * hop,)),
            pltpu.SemaphoreType.DMA((7 * CHUNKS,)), pltpu.SemaphoreType.DMA((7 * CHUNKS,)),
        ],
        compiler_params=pltpu.CompilerParams(
            collective_id=0, has_side_effects=True, vmem_limit_bytes=60 * 1024 * 1024
        ),
    )(
        tokens, gain_attn.reshape(1, width), gain_ffn.reshape(1, width), cosine, sine,
        query_pos, positions,
        w_query, w_key, w_value, w_out, w_gate, w_up, w_down,
    )


def solution(mesh):
    placed = (
        P("blk", None), P(), P(), P(),
        P(None, "tp"), P(None, "tp"), P(None, "tp"), P("tp", None),
        P(None, "tp"), P(None, "tp"), P("tp", None),
    )
    return jax.shard_map(
        functools.partial(local, mesh.shape["blk"]),
        mesh=mesh, in_specs=placed, out_specs=P("blk", "tp"), check_vma=False,
    )
```

time: 171 us -> 58.1 us (0.34)
  waiting for transfers between devices: 100 us -> 0 us
  Pallas kernels: 0 us -> 53.4 us
  matrix products: 34.7 us -> 0 us
  between operations: 13.3 us -> 0.04 us
  other arithmetic: 14.3 us -> 1.93 us
  local copies, waits for them, and re-layouts: 7.5 us -> 2.62 us
    pallas_call x0 -> x1, Pallas kernels: none -> 53.4 us  [local(): pl.pallas_call(functools.partial(kernel, n), out_shape=jax.ShapeDtypeStru...]
    all_gather x1 -> x0, waiting for transfers between devices: 39.3 us -> none  [local(): piece = lax.all_gather(packed, 'blk', axis=0, tiled=True)]
    psum x1 -> x0, waiting for transfers between devices: 35.2 us -> none  [local(): lax.psum(partial_value.astype(jnp.bfloat16), 'tp').astype(jnp.float32)]
    dot_general x14 -> x0, matrix products: 34.7 us -> none  [the longest x1 12.4 us: local(): down = jnp.dot(hidden, w_down, preferred_element_type=jnp.float32)]
    reduce_scatter x1 -> x0, waiting for transfers between devices: 25.4 us -> none  [local(): lax.psum_scatter(down.astype(jnp.bfloat16), 'tp', scatter_dimension=1, ti...]
    reduce_sum x7 -> x0, other arithmetic: 6.58 us -> none  [the longest x4 4.03 us: attend(): denominator = denominator * factor + jnp.sum(weights, axis=-1)]
    slice x4 -> x0, local copies, waits for them, and re-layouts: 3.98 us -> none  [attend(): value_block = block[:, kv_local * HD:].reshape(-1, kv_local, HD)]
    while x20 -> x0, local copies, waits for them, and re-layouts: 3.19 us -> none
  transfers between devices with their start and end apart: 3 -> 0, of which waited for: 3 -> 0; matrix products, arithmetic and copies ran while one was open for 2% -> 0% of each run, Pallas kernels for 0% -> 0%
where the time goes in v1:
time: 58.1 us; the launch traced here: 57.9 us
  Pallas kernels  53.4 us (92%)
  local copies, waits for them, and re-layouts  2.62 us (5%)
  other arithmetic  1.93 us (3%)
    pallas_call x1, Pallas kernels, local(): pl.pallas_call(functools.partial(kernel, n), out_shape=jax.ShapeDtypeStru...  53.4 us
    unnamed x3, local copies, waits for them, and re-layouts  1.67 us
    mul x1, other arithmetic, local(): sine = jnp.sin(angle) * jnp.where(lanes % HD < HD // 2, -1.0, 1.0)[None, :]  1.24 us

profile of v1, /device:TPU:0, one launch (start us, length us, event | category | flops | bytes accessed | tf_op | source)
XLA Modules:
  0.0 57.9 jit_solution(5828731635581821544)
XLA Ops:
  0.0 0.7 %broadcast_multiply_fusion = s32[16]{0:T(128)S(1)} fusion(s32[16]{0:T(128)} %param.12), kind=kLoop, calls=%fused_computation.14 | loop fusion | flops 16 | bytes 128 | tf_op jit(solution)/shard_map/mul | solution.py:311
  0.7 0.1 add.49
  0.7 0.1 add.50
  0.8 0.0 copy-start
  0.9 0.8 %copy.12.qpos = s32[256,1]{1,0:T(8,128)} copy(s32[256,1]{0,1:T(1,128)S(1)} %get-tuple-element.5) | data formatting | bytes 2048 | tf_op jit(solution)/shard_map/reshape | solution.py:315
  1.7 1.2 %fusion = (f32[256,128]{1,0:T(8,128)}, f32[256,128]{1,0:T(8,128)}) fusion(f32[128]{0:T(128)S(1)} %get-tuple-element.9, f32[128]{0:T(128)S(1)} %get-tuple-element.10, f32[256]{0:T(256)S(1)} %bitcast.11), kind=kLoop, calls=%fused_computation.2 | loop fusion | flops 65536 | bytes 264192 | tf_op jit(solution)/shard_map/mul | solution.py:320
  2.9 0.0 copy-done
  2.9 53.4 %shard_map.109 = bf16[256,512]{1,0:T(8,128)(2,1)} custom-call(bf16[256,2048]{1,0:T(8,128)(2,1)} %tokens.1, f32[1,2048]{1,0:T(1,128)} %bitcast.9, f32[1,2048]{1,0:T(1,128)} %bitcast.10, f32[256,128]{1,0:T(8,128)} %get-tuple-element.8.cosine, f32[256,128]{1,0:T(8,128)} %get-tuple-element.7.sine, s32[256,1]{1,0:T(8,128)} %copy.12.qpos, s32[8,1,256]{2,1,0:T(1,128)} %copy-done, ...), custom_call_target="tpu_custom_call" | custom-call | tf_op jit(solution)/shard_map/pallas_call | solution.py:325
  56.3 1.7 %copy.14 = bf16[256,512]{1,0:T(8,128)(2,1)} copy(bf16[256,512]{1,0:T(8,128)(2,1)} %shard_map.109) | data formatting | bytes 524288
  (4 shorter events, 0.0 us)
Async XLA Ops:
  0.8 2.1 %copy-start = (s32[8,1,256]{2,1,0:T(1,128)}, s32[8,1,256]{2,1,0:T(1,128)S(1)}, u32[]{:S(2)}) copy-start(s32[8,1,256]{2,1,0:T(1,128)S(1)} %broadcast_add_fusion.kpos) | copy-start | bytes 24580

commit v2 on v1

--- a/solution.py
+++ b/solution.py
@@ -2,6 +2,7 @@
 
 import jax
 import jax.numpy as jnp
+import numpy as np
 from jax import lax
 from jax.experimental import pallas as pl
 from jax.experimental.pallas import tpu as pltpu
@@ -13,6 +14,7 @@
 MASKED = -1e30
 MESH = pl.DeviceIdType.MESH
 CHUNKS = 2
+PARTS = 4
 BF = jnp.bfloat16
 F32 = jnp.float32
 
@@ -34,7 +36,7 @@
 
 def kernel(
     n,
-    tokens, gain_attn, gain_ffn, cosine, sine, qpos, kpos,
+    order, tokens, gain_attn, gain_ffn, freq, base_cos, base_sin,
     w_query, w_key, w_value, w_out, w_gate, w_up, w_down,
     out,
     wq, wkv, wo, wg, wu, wd,
@@ -80,9 +82,28 @@
     low = lane < 64
     rope_first = (lane % 64) < 32
 
+    turn_rows = rows // 2
+
+    def place_of(b, shape, axis):
+        at = lax.broadcasted_iota(jnp.int32, shape, axis)
+        return jnp.where(
+            at < turn_rows, order[2 * b] * turn_rows + at, (order[2 * b + 1] - 1) * turn_rows + at
+        )
+
+    qpos = place_of(blk, (rows, 1), 0)
+    cos_parts, sin_parts = [], []
+    for h in range(2):
+        start = (order[2 * blk + h] * turn_rows).astype(F32) * freq[...]
+        c0, s0 = jnp.cos(start), jnp.sin(start)
+        cos_parts.append(c0 * base_cos[...] - s0 * base_sin[...])
+        sin_parts.append(s0 * base_cos[...] + c0 * base_sin[...])
+    cosine = jnp.concatenate(cos_parts, axis=0)
+    sine = jnp.concatenate(sin_parts, axis=0)
+    sine = jnp.where(rope_first, -sine, sine)
+
     def rope(u):
         turned = jnp.where(rope_first, pltpu.roll(u, 96, 1), pltpu.roll(u, 32, 1))
-        return u * cosine[...] + turned * sine[...]
+        return u * cosine + turned * sine
 
     first[0].wait()
     first[1].wait()
@@ -107,13 +128,13 @@
     pl.semaphore_wait(barrier, 4)
 
     hop = n // 2
-    hrow = rows // 2
+    hrow = rows // PARTS
 
     def ring_copy(direction, step, part):
         toward = right if direction == 0 else left
         owner = ring_index(place - (step - 1) if direction == 0 else place + (step - 1), n)
         ref = kv.at[owner, pl.ds(part * hrow, hrow)]
-        k = (direction * hop + step - 1) * 2 + part
+        k = (direction * hop + step - 1) * PARTS + part
         return pltpu.make_async_remote_copy(
             src_ref=ref, dst_ref=ref,
             send_sem=ksend.at[k], recv_sem=krecv.at[k],
@@ -123,7 +144,7 @@
     def arrival(direction, step, part):
         owner = ring_index(place - step if direction == 0 else place + step, n)
         ref = kv.at[owner, pl.ds(part * hrow, hrow)]
-        k = (direction * hop + step - 1) * 2 + part
+        k = (direction * hop + step - 1) * PARTS + part
         return pltpu.make_async_remote_copy(
             src_ref=ref, dst_ref=ref,
             send_sem=ksend.at[k], recv_sem=krecv.at[k],
@@ -131,7 +152,7 @@
         )
 
     def used(direction, step, part):
-        return step < hop or part == direction
+        return step < hop or part // (PARTS // 2) == direction
 
     sent = []
 
@@ -141,7 +162,7 @@
             c.start()
             sent.append(c)
 
-    for part in range(2):
+    for part in range(PARTS):
         for direction in range(2):
             send(direction, 1, part)
 
@@ -156,9 +177,15 @@
             keep = low if upper == 0 else jnp.logical_not(low)
             q_v[j] = jnp.where(keep, picked, 0.0).astype(BF)
 
-    def attend(blocks, fresh):
+    def pump(step, part):
+        for direction in range(2):
+            if step <= hop and used(direction, step, part):
+                arrival(direction, step, part).wait_recv()
+                send(direction, step + 1, part)
+
+    def attend(blocks, fresh, later):
         biases = [
-            jnp.where(kpos[b] <= qpos[...], 0.0, MASKED).astype(F32) for b in blocks
+            jnp.where(place_of(b, (1, rows), 1) <= qpos, 0.0, MASKED).astype(F32) for b in blocks
         ]
         ones = jnp.ones((rows, 128), BF)
 
@@ -191,18 +218,13 @@
             else:
                 acc[j] = acc[j] * jnp.exp(old - newest) + total
             m_v[j] = newest
-
-    attend([blk], True)
-    for step in range(1, hop + 1):
-        for part in range(2):
-            for direction in range(2):
-                if used(direction, step, part):
-                    arrival(direction, step, part).wait_recv()
-                    send(direction, step + 1, part)
-        if step < hop:
-            attend([ring_index(place - step, n), ring_index(place + step, n)], False)
-        else:
-            attend([ring_index(place + step, n)], False)
+            if (j + 1) % (n_heads // PARTS) == 0:
+                pump(later, (j + 1) // (n_heads // PARTS) - 1)
+
+    attend([blk], True, 1)
+    for step in range(1, hop):
+        attend([ring_index(place - step, n), ring_index(place + step, n)], False, step + 1)
+    attend([ring_index(place + hop, n)], False, hop + 1)
 
     for g in range(group):
         a, b = acc[g], acc[group + g]
@@ -282,12 +304,12 @@
             rest_ffn[2].wait()
         rs_send[0, s] = dot(hidden[s], wd[:, quarter(1 - xx, 1 - core)]).astype(BF)
         down_far[c].start()
+        rs_send[1, s] = dot(hidden[s], wd[:, quarter(xx, 1 - core)]).astype(BF)
+        down_near[c].start()
         own = dot(hidden[s], wd[:, quarter(1 - xx, core)]).astype(BF).astype(F32)
         down_far[c].wait_recv()
         xs_send[s] = (own + rs_recv[0, s].astype(F32)).astype(BF)
         down_cross[c].start()
-        rs_send[1, s] = dot(hidden[s], wd[:, quarter(xx, 1 - core)]).astype(BF)
-        down_near[c].start()
         own = dot(hidden[s], wd[:, quarter(xx, core)]).astype(BF).astype(F32)
         down_near[c].wait_recv()
         fin[s] = resid[s, quarter(xx, core)] + (own + rs_recv[1, s].astype(F32))
@@ -308,16 +330,10 @@
     n_heads = inner // HD
     ffn = w_gate.shape[1]
     count = n * rows
-    positions = (order[:, None] * half_rows + jnp.arange(half_rows, dtype=jnp.int32)[None, :]).reshape(
-        n, 1, rows
-    )
-    blk = lax.axis_index("blk")
-    query_pos = lax.dynamic_slice_in_dim(positions, blk, 1, 0).reshape(rows, 1)
-    lanes = jnp.arange(128, dtype=jnp.int32)
-    freq = ROPE_BASE ** (-((lanes % 32).astype(F32) * 2.0 / HD))
-    angle = query_pos.astype(F32) * freq[None, :]
-    cosine = jnp.cos(angle)
-    sine = jnp.sin(angle) * jnp.where((lanes % HD) < HD // 2, -1.0, 1.0)[None, :]
+    lanes = np.arange(128)
+    freq = (ROPE_BASE ** (-((lanes % 32) * 2.0 / HD))).astype(np.float32)
+    base = np.arange(half_rows)[:, None] * freq[None, :].astype(np.float64)
+    base_cos, base_sin = np.cos(base).astype(np.float32), np.sin(base).astype(np.float32)
     vmem = pl.BlockSpec(memory_space=pltpu.VMEM)
     hbm = pl.BlockSpec(memory_space=pl.ANY)
     V = pltpu.VMEM
@@ -325,7 +341,7 @@
     return pl.pallas_call(
         functools.partial(kernel, n),
         out_shape=jax.ShapeDtypeStruct((rows, width // 4), BF),
-        in_specs=[vmem] * 7 + [hbm] * 7,
+        in_specs=[pl.BlockSpec(memory_space=pltpu.SMEM)] + [vmem] * 6 + [hbm] * 7,
         out_specs=vmem,
         scratch_shapes=[
             V((width, inner), BF), V((width, 256), BF), V((inner, width), BF),
@@ -340,15 +356,15 @@
             V((2, rows, width // 4), BF), V((2, rows, width // 4), BF),
             V((rows, width // 4), BF), V((rows, width // 4), BF),
             pltpu.SemaphoreType.DMA((6 + n_heads,)),
-            pltpu.SemaphoreType.DMA((4 * hop,)), pltpu.SemaphoreType.DMA((4 * hop,)),
+            pltpu.SemaphoreType.DMA((2 * PARTS * hop,)), pltpu.SemaphoreType.DMA((2 * PARTS * hop,)),
             pltpu.SemaphoreType.DMA((7 * CHUNKS,)), pltpu.SemaphoreType.DMA((7 * CHUNKS,)),
         ],
         compiler_params=pltpu.CompilerParams(
             collective_id=0, has_side_effects=True, vmem_limit_bytes=60 * 1024 * 1024
         ),
     )(
-        tokens, gain_attn.reshape(1, width), gain_ffn.reshape(1, width), cosine, sine,
-        query_pos, positions,
+        order, tokens, gain_attn.reshape(1, width), gain_ffn.reshape(1, width),
+        jnp.asarray(freq[None, :]), jnp.asarray(base_cos), jnp.asarray(base_sin),
         w_query, w_key, w_value, w_out, w_gate, w_up, w_down,
     )
 

time: 58.1 us -> 54.5 us (0.938)
  other arithmetic: 1.93 us -> 0 us
  local copies, waits for them, and re-layouts: 2.62 us -> 1.67 us
  Pallas kernels: 53.4 us -> 52.6 us
    mul x2 -> x0, other arithmetic: 1.9 us -> none  [the longest x1 1.24 us: local(): sine = jnp.sin(angle) * jnp.where(lanes % HD < HD // 2, -1.0, 1.0)[None, :]]
    reshape x1 -> x0, local copies, waits for them, and re-layouts: 0.79 us -> none  [local(): query_pos = lax.dynamic_slice_in_dim(positions, blk, 1, 0).reshape(rows, 1)]
    pallas_call x1, Pallas kernels: 53.4 us -> 52.6 us  [local(): pl.pallas_call(functools.partial(kernel, n), out_shape=jax.ShapeDtypeStru...]
    unnamed x3 -> x1, local copies, waits for them, and re-layouts: 1.67 us -> 1.67 us
where the time goes in v2:
time: 54.5 us; the launch traced here: 54.3 us
  Pallas kernels  52.6 us (97%)
  local copies, waits for them, and re-layouts  1.67 us (3%)
    pallas_call x1, Pallas kernels, local(): pl.pallas_call(functools.partial(kernel, n), out_shape=jax.ShapeDtypeStru...  52.6 us
    unnamed x1, local copies, waits for them, and re-layouts  1.67 us

profile of v2, /device:TPU:0, one launch (start us, length us, event | category | flops | bytes accessed | tf_op | source)
XLA Modules:
  0.0 54.3 jit_solution(10800489411931713445)
XLA Ops:
  0.0 52.6 %shard_map.136 = bf16[256,512]{1,0:T(8,128)(2,1)} custom-call(s32[16]{0:T(128)} %order.1, bf16[256,2048]{1,0:T(8,128)(2,1)} %tokens.1, f32[1,2048]{1,0:T(1,128)} %bitcast.2, f32[1,2048]{1,0:T(1,128)} %bitcast.3, f32[1,128]{1,0:T(1,128)} %constant.6.clone.freq, f32[128,128]{1,0:T(8,128)} %constant.7.clone.base_cos, f32[128,128]{1,0:T(8,128)} %constant.8.clone.base_sin, ...), custom_call_target="tpu_custom_call" | custom-call | tf_op jit(solution)/shard_map/pallas_call | solution.py:341
  52.6 1.7 %copy.16 = bf16[256,512]{1,0:T(8,128)(2,1)} copy(bf16[256,512]{1,0:T(8,128)(2,1)} %shard_map.136) | data formatting | bytes 524288
